TPU v7x, 32 devices: a whole 2x2x4 slice. The times are simulated.
32 devices in a mesh: role: 2 (over x), dp: 4 (over y, core), ctx: 4 (over z).
Axes of the slice: x: 2, y: 2, z: 4, core: 2. Of those that a mesh axis runs over, the one named last changes fastest.
Arguments:
- teacher_states: bfloat16 [4, 512, 5120], P('dp', 'ctx'), may hold values from -50 to 50
- student_states: bfloat16 [4, 512, 3584], P('dp', 'ctx'), may hold values from -50 to 50
- teacher_gain: float32 [5120], replicated, may hold values from 0.25 to 1.75
- student_gain: float32 [3584], replicated, may hold values from 0.25 to 1.75
- mentor_output_weights: bfloat16 [4, 5120, 2048], P(None, None, 'ctx'), may hold values from -2 to 2
- student_heads: bfloat16 [4, 3584, 2048], P(None, None, 'ctx'), may hold values from -2 to 2
- segments: int32 [4, 512], P('dp', 'ctx'), may hold values from 0 to 7, never falling along the last dimension, each value on 1 to 256 neighbouring positions
- targets: int32 [4, 512, 4], P('dp', 'ctx'), may hold values from 0 to 2047
Outputs:
- grad_heads: float32 [4, 3584, 2048], P(None, ('role', 'dp'), 'ctx')
- frame_terms: float32 [2, 4, 512, 4], P('role', 'dp', 'ctx')
All inputs are finite; a program needn't handle non-finite values.
Results may differ from a plain program's by a relative error of at most 0.0048.
Values may be sent and summed in bfloat16 or wider, within the bound.
A program may use at most 192 MiB of HBM per device.

v0:
```python
import jax
import jax.numpy as jnp
from jax import lax
from jax.sharding import PartitionSpec as P

QUANTIZER_TOTAL = 4
MBATCH = 4
epsilon = 1e-06
sharpness_divisor = 2.0
blend_ratio = 0.5


def shifted(value, axis, steps):
    count = lax.axis_size(axis)
    initial, last = (max(0, -steps), min(count, count - steps))
    return lax.ppermute(value, axis, [(source, source + steps) for source in range(initial, last)])


def normalize(states, gain):
    values = states.astype(jnp.float32)
    factor = lax.rsqrt(jnp.mean(values * values, axis=-1, keepdims=True) + epsilon)
    return (values * factor * gain).astype(jnp.bfloat16)


def on_device(
    teacher_states,
    student_states,
    teacher_gain,
    student_gain,
    mentor_output_weights,
    student_heads,
    segments,
    targets,
):
    columns = mentor_output_weights.shape[2]
    ctx_count = lax.axis_size("ctx")
    ctx_rank = lax.axis_index("ctx")
    col_start = ctx_rank * columns
    rows_here = teacher_states.shape[1]
    batch_rows = rows_here // MBATCH
    group_rows = batch_rows * ctx_count
    all_segments, all_targets = (
        lax.all_gather(segments, "ctx", axis=1, tiled=True),
        lax.all_gather(targets, "ctx", axis=1, tiled=True),
    )
    length = all_segments.shape[1]
    documents = 2 * ctx_count
    members = (all_segments[0][None, :] == jnp.arange(documents, dtype=jnp.int32)[:, None]).astype(
        jnp.float32
    )
    counts = jnp.sum(members, axis=1)
    row_sizes = jnp.dot(counts, members, precision=lax.Precision.HIGHEST)
    weights = length / (documents * row_sizes)
    own_targets = all_targets[0] - col_start
    is_teacher = lax.axis_index("role") == 0
    positions = jnp.arange(columns)

    def per_batch(values, batch_index):
        trailing = values.shape[1:]
        return values.reshape((ctx_count, MBATCH, batch_rows) + trailing)[:, batch_index].reshape(
            (group_rows,) + trailing
        )

    gradient = jnp.zeros((QUANTIZER_TOTAL, student_heads.shape[1], columns), jnp.float32)
    frame_parts = []
    blocks = []
    teacher_parts = []
    for batch_index in range(MBATCH):
        teacher_local_rows = normalize(
            teacher_states[0, batch_index * batch_rows : (batch_index + 1) * batch_rows],
            teacher_gain,
        )
        scaled = (
            lax.cond(
                is_teacher,
                lambda piece: jnp.einsum(
                    "rd,qdc->rqc", piece, mentor_output_weights, preferred_element_type=jnp.float32
                ),
                lambda piece: jnp.zeros((piece.shape[0], QUANTIZER_TOTAL, columns), jnp.float32),
                lax.all_gather(teacher_local_rows, "ctx", axis=0, tiled=True),
            )
            / sharpness_divisor
        )
        teacher_local_peak = jnp.max(scaled, axis=2)
        teacher_largest_activation = lax.pmax(teacher_local_peak, "ctx")
        totals = lax.psum(
            jnp.sum(jnp.exp(scaled - teacher_largest_activation[:, :, None]), axis=2), "ctx"
        )
        log_probs = scaled - (teacher_largest_activation + jnp.log(totals))[:, :, None]
        teacher_hits = positions[None, None, :] == per_batch(own_targets, batch_index)[:, :, None]
        picked = -jnp.sum(jnp.where(teacher_hits, log_probs, 0.0), axis=2)
        teacher_terms = lax.psum_scatter(picked, "ctx", scatter_dimension=0, tiled=True)
        block = log_probs.astype(jnp.bfloat16)
        blocks.append(block)
        teacher_parts.append(teacher_terms)
    arrived = shifted(jnp.stack(blocks), "role", 1)
    for batch_index in range(MBATCH):
        received = arrived[batch_index]
        student_gradient = gradient
        local_rows = normalize(
            student_states[0, batch_index * batch_rows : (batch_index + 1) * batch_rows],
            student_gain,
        )
        gathered = lax.all_gather(local_rows, "ctx", axis=0, tiled=True)
        raw_activation_grid = lax.cond(
            is_teacher,
            lambda rows: jnp.zeros((rows.shape[0], QUANTIZER_TOTAL, columns), jnp.float32),
            lambda rows: jnp.einsum(
                "rd,qdc->rqc", rows, student_heads, preferred_element_type=jnp.float32
            ),
            gathered,
        )
        local_peak = jnp.max(raw_activation_grid, axis=2)
        largest_activation = lax.pmax(local_peak, "ctx")
        centered_activations = raw_activation_grid - largest_activation[:, :, None]
        plain, warmed_totals = lax.psum(
            (
                jnp.sum(jnp.exp(centered_activations), axis=2),
                jnp.sum(jnp.exp(centered_activations / sharpness_divisor), axis=2),
            ),
            "ctx",
        )
        untempered_logdensity = (
            raw_activation_grid - (largest_activation + jnp.log(plain))[:, :, None]
        )
        warmed_logdensity = (
            raw_activation_grid / sharpness_divisor
            - (largest_activation / sharpness_divisor + jnp.log(warmed_totals))[:, :, None]
        )
        teacher_logp = received.astype(jnp.float32)
        mentor_distribution = jnp.exp(teacher_logp)
        hits = (positions[None, None, :] == per_batch(own_targets, batch_index)[:, :, None]).astype(
            jnp.float32
        )
        kullback_gap = jnp.sum(mentor_distribution * (teacher_logp - warmed_logdensity), axis=2)
        mismatch_penalty = -jnp.sum(hits * untempered_logdensity, axis=2)
        loss_values = (
            blend_ratio * sharpness_divisor * sharpness_divisor * kullback_gap
            + (1.0 - blend_ratio) * mismatch_penalty
        )
        terms = lax.psum_scatter(loss_values, "ctx", scatter_dimension=0, tiled=True)
        gradient_scaling = per_batch(weights, batch_index)[:, None, None] * (
            blend_ratio * sharpness_divisor * (jnp.exp(warmed_logdensity) - mentor_distribution)
            + (1.0 - blend_ratio) * (jnp.exp(untempered_logdensity) - hits)
        )
        gradient_scaling = gradient_scaling.astype(jnp.bfloat16)
        student_gradient = lax.cond(
            is_teacher,
            lambda total: total,
            lambda total: total
            + jnp.einsum(
                "rd,rqc->qdc", gathered, gradient_scaling, preferred_element_type=jnp.float32
            ),
            student_gradient,
        )
        gradient = student_gradient
        frame_parts.append(jnp.where(is_teacher, teacher_parts[batch_index], terms))
    shares = lax.psum_scatter(gradient, ("role", "dp"), scatter_dimension=1, tiled=True)
    frame_terms = jnp.concatenate(frame_parts, axis=0).reshape(1, 1, rows_here, QUANTIZER_TOTAL)
    return (shares, frame_terms)


def solution(mesh):
    return jax.shard_map(
        on_device,
        mesh=mesh,
        in_specs=(
            P("dp", "ctx", None),
            P("dp", "ctx", None),
            P(),
            P(),
            P(None, None, "ctx"),
            P(None, None, "ctx"),
            P("dp", "ctx"),
            P("dp", "ctx", None),
        ),
        out_specs=(P(None, ("role", "dp"), "ctx"), P("role", "dp", "ctx", None)),
        check_vma=False,
    )
```

profile of v0, /device:TPU:0, one launch (start us, length us, event | category | flops | bytes accessed | tf_op | source)
XLA Modules:
  0.0 620.6 jit_solution(17266748540502973690)
XLA Ops:
  7.2 1.7 fusion.44
  8.9 2.6 fusion.46
  13.7 1.6 fusion.69
  15.3 1.6 fusion.71
  16.9 35.9 %all_gather.38 = bf16[128,3584]{1,0:T(8,128)(2,1)} all-gather(bf16[32,3584]{1,0:T(8,128)(2,1)S(1)} %get-tuple-element.195), channel_id=1, replica_groups=mesh['role'=2,'dp'=4,'ctx'=4] {'ctx'}, dimensions={0}, use_global_device_ids=true | all-gather | bytes 1146880 | tf_op jit(solution)/shard_map/all_gather | solution.py:104
  52.7 24.2 %all_gather.31 = bf16[128,3584]{1,0:T(8,128)(2,1)} all-gather(bf16[32,3584]{1,0:T(8,128)(2,1)S(1)} %get-tuple-element.196), channel_id=1, replica_groups=mesh['role'=2,'dp'=4,'ctx'=4] {'ctx'}, dimensions={0}, use_global_device_ids=true | all-gather | bytes 1146880 | tf_op jit(solution)/shard_map/all_gather | solution.py:104
  77.1 1.4 copy.61
  79.2 32.3 %all_gather.37 = bf16[128,3584]{1,0:T(8,128)(2,1)} all-gather(bf16[32,3584]{1,0:T(8,128)(2,1)S(1)} %get-tuple-element.194), channel_id=1, replica_groups=mesh['role'=2,'dp'=4,'ctx'=4] {'ctx'}, dimensions={0}, use_global_device_ids=true | all-gather | bytes 1146880 | tf_op jit(solution)/shard_map/all_gather | solution.py:104
  111.8 1.3 copy.68
  113.2 31.1 %all_gather.39 = bf16[128,3584]{1,0:T(8,128)(2,1)} all-gather(bf16[32,3584]{1,0:T(8,128)(2,1)S(1)} %get-tuple-element.193), channel_id=1, replica_groups=mesh['role'=2,'dp'=4,'ctx'=4] {'ctx'}, dimensions={0}, use_global_device_ids=true | all-gather | bytes 1146880 | tf_op jit(solution)/shard_map/all_gather | solution.py:104
  144.9 12.5 %all_gather.36 = s32[1,512,4]{1,2,0:T(4,128)S(1)} all-gather(s32[1,128,4]{1,2,0:T(4,128)S(1)} %copy-done.6), channel_id=1, replica_groups=mesh['role'=2,'dp'=4,'ctx'=4] {'ctx'}, dimensions={1}, use_global_device_ids=true | all-gather | bytes 10240 | tf_op jit(solution)/shard_map/all_gather | solution.py:44
  158.0 13.0 %conditional.14 = (f32[128,4,512]{0,2,1:T(8,128)S(1)}) conditional(s32[]{:T(128)} %convert_element_type.149, () %tuple.84, (bf16[128,5120]{1,0:T(8,128)(2,1)}, bf16[4,5120,512]{2,1,0:T(8,128)(2,1)}) %tuple.85), branch_computations={%region_16.17_spmd, %region_17.18_spmd} | conditional | flops 2684354560 | bytes 23330824 | solution.py:74
  158.1 12.8 %fusion.4 = f32[128,4,512]{0,2,1:T(8,128)S(1)} fusion(bf16[4,5120,512]{2,1,0:T(8,128)(2,1)} %get-tuple-element.93, bf16[128,5120]{1,0:T(8,128)(2,1)} %get-tuple-element.92), kind=kOutput, calls=%fused_computation.4 | convolution fusion | flops 2684354560 | bytes 23330816 | tf_op jit(solution)/shard_map/cond | solution.py:74
  171.0 13.9 %conditional.15 = (f32[128,4,512]{0,2,1:T(8,128)}) conditional(s32[]{:T(128)} %convert_element_type.149, () %tuple.86, (bf16[128,5120]{1,0:T(8,128)(2,1)}, bf16[4,5120,512]{2,1,0:T(8,128)(2,1)}) %tuple.87), branch_computations={%region_23.24_spmd, %region_24.25_spmd} | conditional | flops 2684354560 | bytes 23330824 | solution.py:74
  171.0 13.8 %fusion.6 = f32[128,4,512]{0,2,1:T(8,128)} fusion(bf16[4,5120,512]{2,1,0:T(8,128)(2,1)} %get-tuple-element.95, bf16[128,5120]{1,0:T(8,128)(2,1)} %get-tuple-element.94), kind=kOutput, calls=%fused_computation.6 | convolution fusion | flops 2684354560 | bytes 23330816 | tf_op jit(solution)/shard_map/cond | solution.py:74
  184.9 12.9 %conditional.16 = (f32[128,4,512]{0,2,1:T(8,128)S(1)}) conditional(s32[]{:T(128)} %convert_element_type.149, () %tuple.88, (bf16[128,5120]{1,0:T(8,128)(2,1)}, bf16[4,5120,512]{2,1,0:T(8,128)(2,1)}) %tuple.89), branch_computations={%region_30.31_spmd, %region_31.32_spmd} | conditional | flops 2684354560 | bytes 23330824 | solution.py:74
  184.9 12.7 %fusion.8 = f32[128,4,512]{0,2,1:T(8,128)S(1)} fusion(bf16[4,5120,512]{2,1,0:T(8,128)(2,1)} %get-tuple-element.102, bf16[128,5120]{1,0:T(8,128)(2,1)} %get-tuple-element.100), kind=kOutput, calls=%fused_computation.8 | convolution fusion | flops 2684354560 | bytes 23330816 | tf_op jit(solution)/shard_map/cond | solution.py:74
  197.8 1.0 copy-done.2
  198.9 1.3 multiply_reduce_fusion.1
  200.3 12.8 %conditional.13 = (f32[128,4,512]{0,2,1:T(8,128)S(1)}) conditional(s32[]{:T(128)} %convert_element_type.149, () %tuple.82, (bf16[128,5120]{1,0:T(8,128)(2,1)}, bf16[4,5120,512]{2,1,0:T(8,128)(2,1)}) %tuple.83), branch_computations={%region_9.10_spmd, %region_10.11_spmd} | conditional | flops 2684354560 | bytes 23330824 | solution.py:74
  200.3 12.8 %fusion.2 = f32[128,4,512]{0,2,1:T(8,128)S(1)} fusion(bf16[4,5120,512]{2,1,0:T(8,128)(2,1)} %get-tuple-element.90, bf16[128,5120]{1,0:T(8,128)(2,1)} %get-tuple-element.85), kind=kOutput, calls=%fused_computation.2 | convolution fusion | flops 2684354560 | bytes 23330816 | tf_op jit(solution)/shard_map/cond | solution.py:74
  213.1 1.0 copy-done.3
  214.2 17.6 %all-reduce.1 = (f32[128,4]{0,1:T(4,128)S(1)}, f32[128,4]{0,1:T(4,128)S(1)}, f32[128,4]{0,1:T(4,128)S(1)}, f32[128,4]{0,1:T(4,128)S(1)}, f32[128,4]{0,1:T(4,128)...) all-reduce(f32[128,4]{0,1:T(4,128)S(1)} %reduce_max.72, ...), channel_id=1, replica_groups=mesh['role'=2,'dp'=4,'ctx'=4] {'ctx'}, use_global_device_ids=true, to_apply=%region_5.0 | all-reduce | flops 4096 | bytes 32768 | tf_op jit(solution)/shard_map/pmax | solution.py:114
  231.8 1.4 exponential_reduce_fusion.7
  233.2 1.4 exponential_reduce_fusion.8
  234.6 1.4 exponential_reduce_fusion.9
  236.1 1.4 exponential_reduce_fusion.10
  237.5 1.5 exponential_reduce_fusion.11
  239.9 15.7 %all-reduce = (f32[128,4]{0,1:T(4,128)S(1)}, f32[128,4]{0,1:T(4,128)S(1)}, f32[128,4]{0,1:T(4,128)S(1)}, f32[128,4]{0,1:T(4,128)S(1)}, f32[128,4]{0,1:T(4,128)S(...) all-reduce(f32[128,4]{0,1:T(4,128)S(1)} %get-tuple-element.141, ...), channel_id=1, replica_groups=mesh['role'=2,'dp'=4,'ctx'=4] {'ctx'}, use_global_device_ids=true, to_apply=%region_37.38 | all-reduce | flops 6144 | bytes 49152 | tf_op jit(solution)/shard_map/psum | solution.py:116
  255.7 1.5 select_reduce_fusion.5
  257.2 1.5 select_reduce_fusion.3
  258.6 1.5 select_reduce_fusion.1
  260.1 1.6 select_reduce_fusion.6
  261.6 1.6 pad_maximum_fusion
  263.2 2.6 collective-permute-start
  265.9 9.4 %all_gather.30 = s32[1,512]{1,0:T(1,128)S(1)} all-gather(s32[1,128]{1,0:T(1,128)S(1)} %copy-done.7), channel_id=1, replica_groups=mesh['role'=2,'dp'=4,'ctx'=4] {'ctx'}, dimensions={1}, use_global_device_ids=true | all-gather | bytes 2560 | tf_op jit(solution)/shard_map/all_gather | solution.py:43
  275.4 0.7 copy.78
  276.4 0.7 copy.90
  277.3 0.7 copy.86
  278.5 0.7 copy.82
  279.3 17.3 %collective-permute-done = bf16[4,128,4,512]{1,3,2,0:T(8,128)(2,1)} collective-permute-done((bf16[4,128,4,512]{1,3,2,0:T(8,128)(2,1)}, bf16[4,128,4,512]{1,3,2,0:T(8,128)(2,1)}, u32[]{:S(2)}, u32[]{:S(2)}) %collective-permute-start) | collective-permute-done | bytes 2097184 | tf_op jit(solution)/shard_map/ppermute | solution.py:16
  296.6 3.7 fusion.43
  300.3 0.7 copy.92
  301.1 0.7 copy.88
  301.9 0.7 copy.84
  303.9 4.2 fusion.42
  308.1 2.0 fusion.30
  310.1 13.5 %conditional.20 = (f32[4,3584,512]{1,2,0:T(8,128)}) conditional(s32[]{:T(128)} %convert_element_type.149, (bf16[128,4,512]{0,2,1:T(8,128)(2,1)S(1)}, bf16[128,3584]{1,0:T(8,128)(2,1)}) %tuple.96, () %tuple.97), branch_computations={%region_65.66_spmd, %region_66.67_spmd} | conditional | flops 1879048192 | bytes 30801928 | solution.py:147
  310.1 13.4 %broadcast_in_dim.6 = f32[4,3584,512]{1,2,0:T(8,128)} broadcast(f32[]{:T(128)} %constant.65.clone), dimensions={} | broadcast | bytes 29360132 | tf_op jit(solution)/shard_map/broadcast_in_dim | solution.py:64
  323.6 1.0 copy-done.4
  324.8 27.6 %copy.77 = f32[4,3584,512]{2,1,0:T(8,128)} copy(f32[4,3584,512]{1,2,0:T(8,128)} %get-tuple-element.228) | data formatting | bytes 58720256 | tf_op jit(solution)/shard_map/cond | solution.py:147
  352.4 0.8 copy.79
  353.2 0.8 copy.91
  354.0 0.8 copy.87
  354.8 0.8 copy.83
  355.6 16.0 %reduce-scatter.42.cloned.1.call-done = f32[32,4]{1,0:T(8,128)} async-done(((f32[128,4]{1,0:T(8,128)}), f32[32,4]{1,0:T(8,128)}) %reduce-scatter.42.cloned.1.call-update) | async-done | bytes 528
  371.7 0.8 copy.93
  372.5 18.8 %reduce-scatter.38.cloned.1.call-done = f32[32,4]{1,0:T(8,128)} async-done(((f32[128,4]{1,0:T(8,128)}), f32[32,4]{1,0:T(8,128)}) %reduce-scatter.38.cloned.1.call-update) | async-done | bytes 528
  391.2 0.8 copy.89
  392.0 18.9 %reduce-scatter.34.cloned.1.call-done = f32[32,4]{1,0:T(8,128)} async-done(((f32[128,4]{1,0:T(8,128)}), f32[32,4]{1,0:T(8,128)}) %reduce-scatter.34.cloned.1.call-update) | async-done | bytes 528
  411.0 0.8 copy.85
  411.8 18.8 %reduce-scatter.30.cloned.1.call-done = f32[32,4]{1,0:T(8,128)} async-done(((f32[128,4]{1,0:T(8,128)}), f32[32,4]{1,0:T(8,128)}) %reduce-scatter.30.cloned.1.call-update) | async-done | bytes 528
  430.5 0.8 copy.81
  432.0 181.9 %reduce-scatter.26.cloned.1.call-done = f32[4,448,512]{2,1,0:T(8,128)} async-done(((f32[4,3584,512]{2,1,0:T(8,128)}), f32[4,448,512]{2,1,0:T(8,128)}) %reduce-scatter.26.cloned.1.call-update) | async-done | bytes 3670032 | tf_op jit(solution)/shard_map/reduce_scatter | solution.py:158
  (112 shorter events, 9.4 us)
Async XLA Ops:
  7.2 150.8 %all-gather.7.cloned.1.call-start = ((), (), s32[]{:S(2)}) async-start(), calls=%async_computation.10 | async-start | bytes 1638400 | tf_op jit(solution)/shard_map/all_gather | solution.py:80
  11.5 159.4 %all-gather.9.cloned.1.call-start = ((), (), s32[]{:S(2)}) async-start(), calls=%async_computation.11 | async-start | bytes 1638400 | tf_op jit(solution)/shard_map/all_gather | solution.py:80
  12.3 172.6 %all-gather.11.cloned.1.call-start = ((), (), s32[]{:S(2)}) async-start(), calls=%async_computation.12 | async-start | bytes 1638400 | tf_op jit(solution)/shard_map/all_gather | solution.py:80
  13.0 187.3 %all-gather.5.cloned.1.call-start = ((), (), s32[]{:S(2)}) async-start(), calls=%async_computation.9 | async-start | bytes 1638400 | tf_op jit(solution)/shard_map/all_gather | solution.py:80
  13.6 338.8 %reduce-scatter.28.cloned.1.call-start = ((), (), s32[]{:S(2)}) async-start(), calls=%async_computation.14 | async-start | bytes 81920
  111.7 33.3 %copy-start.6 = (s32[1,128,4]{1,2,0:T(4,128)S(1)}, s32[1,128,4]{1,2,0:T(4,128)}, u32[]{:S(2)}) copy-start(s32[1,128,4]{1,2,0:T(4,128)} %param.39) | copy-start | bytes 6148
  171.0 29.2 %copy-start.1 = (f32[128,4,512]{0,2,1:T(8,128)}, f32[128,4,512]{0,2,1:T(8,128)S(1)}, u32[]{:S(2)}) copy-start(f32[128,4,512]{0,2,1:T(8,128)S(1)} %get-tuple-element.123) | copy-start | bytes 3145732
  197.8 1.0 copy-start.2
  200.3 38.7 %copy-start = (f32[128,4,512]{0,2,1:T(8,128)S(1)}, f32[128,4,512]{0,2,1:T(8,128)}, u32[]{:S(2)}) copy-start(f32[128,4,512]{0,2,1:T(8,128)} %copy.68) | copy-start | bytes 3145732
  213.1 1.0 copy-start.3
  213.1 52.7 %copy-start.7 = (s32[1,128]{1,0:T(1,128)S(1)}, s32[1,128]{1,0:T(1,128)}, u32[]{:S(2)}) copy-start(s32[1,128]{1,0:T(1,128)} %param.38) | copy-start | bytes 1540
  263.2 33.4 %collective-permute-start = (bf16[4,128,4,512]{1,3,2,0:T(8,128)(2,1)}, bf16[4,128,4,512]{1,3,2,0:T(8,128)(2,1)}, u32[]{:S(2)}, u32[]{:S(2)}) collective-permute-start(bf16[4,128,4,512]{1,3,2,0:T(8,128)(2,1)} %pad_maximum_fusion), channel_id=1, source_target_pairs={{0,16},{1,17},{2,18},{3,19},{4,20},{5,21},{6,22},{7,23},{8,24},{9,... | collective-permute-start | bytes 6291464 | tf_op jit(solution)/shard_map/ppermute | solution.py:16
  276.2 77.0 %reduce-scatter.40.cloned.1.call-start = ((), (), s32[]{:S(2)}) async-start(), calls=%async_computation.20 | async-start | bytes 81920
  277.1 76.9 %reduce-scatter.36.cloned.1.call-start = ((), (), s32[]{:S(2)}) async-start(), calls=%async_computation.18 | async-start | bytes 81920
  278.0 76.8 %reduce-scatter.32.cloned.1.call-start = ((), (), s32[]{:S(2)}) async-start(), calls=%async_computation.16 | async-start | bytes 81920
  279.2 92.5 %reduce-scatter.42.cloned.1.call-start = ((), (), s32[]{:S(2)}) async-start(), calls=%async_computation.21 | async-start | bytes 81920
  301.0 90.2 %reduce-scatter.38.cloned.1.call-start = ((), (), s32[]{:S(2)}) async-start(), calls=%async_computation.19 | async-start | bytes 81920
  301.8 109.1 %reduce-scatter.34.cloned.1.call-start = ((), (), s32[]{:S(2)}) async-start(), calls=%async_computation.17 | async-start | bytes 81920
  302.7 127.9 %reduce-scatter.30.cloned.1.call-start = ((), (), s32[]{:S(2)}) async-start(), calls=%async_computation.15 | async-start | bytes 81920
  303.5 310.5 %reduce-scatter.26.cloned.1.call-start = ((), (), s32[]{:S(2)}) async-start(), calls=%async_computation.13 | async-start | bytes 33030144 | tf_op jit(solution)/shard_map/reduce_scatter | solution.py:158
  310.1 13.5 %copy-start.5 = (bf16[128,4,512]{0,2,1:T(8,128)(2,1)S(1)}, bf16[128,4,512]{0,2,1:T(8,128)(2,1)}, u32[]{:S(2)}) copy-start(bf16[128,4,512]{0,2,1:T(8,128)(2,1)} %get-tuple-element.180) | copy-start | bytes 1572868
  323.6 1.0 copy-start.4
Sparse Core Ops, SparseCore 0:
  11.7 49.2 all-gather.6
  62.5 45.3 all-gather.8
  109.5 42.2 all-gather.10
  153.2 34.2 all-gather.4
  276.3 16.5 reduce-scatter.27
  295.0 17.4 reduce-scatter.39
  314.7 17.4 reduce-scatter.35
  334.5 17.4 reduce-scatter.31
  354.2 17.4 reduce-scatter.41
  373.8 17.4 reduce-scatter.37
  393.5 17.4 reduce-scatter.33
  413.1 17.4 reduce-scatter.29
  434.7 179.1 reduce-scatter.25
where the time goes:
time: 630 us; the launch traced here: 621 us
  waiting for transfers between devices  274 us (43%)
  blocking collectives  179 us (28%)
  local copies, waits for them, and re-layouts  61.1 us (10%)
  matrix products  52.3 us (8%)
  other arithmetic  36 us (6%)
  between operations  14.5 us (2%)
    reduce_scatter x1, waiting for transfers between devices, on_device(): lax.psum_scatter(gradient, ('role', 'dp'), scatter_dimension=1, tiled=True)  182 us
    all_gather x4, blocking collectives, on_device(): gathered = lax.all_gather(local_rows, 'ctx', axis=0, tiled=True)  124 us
    unnamed x21, waiting for transfers between devices  74.6 us
    cond x4, matrix products, on_device(): lax.cond(is_teacher, lambda piece: jnp.einsum('rd,qdc->rqc', piece, mento...  52.2 us
    cond x1, local copies, waits for them, and re-layouts, on_device(): lax.cond(is_teacher, lambda total: total, lambda total: total + jnp.einsu...  27.6 us
    pmax x1, blocking collectives, on_device(): largest_activation = lax.pmax(local_peak, 'ctx')  17.6 us
    ppermute x1, waiting for transfers between devices, shifted(): lax.ppermute(value, axis, [(source, source + steps) for source in range(i...  17.3 us
    psum x1, blocking collectives, on_device(): lax.psum((jnp.sum(jnp.exp(centered_activations), axis=2), jnp.sum(jnp.exp...  15.7 us
  transfers between devices with their start and end apart: 14, of which 6 were waited for; matrix products, arithmetic and copies ran while one was open for 18% of the time, Pallas kernels for 0%

commit v1 on v0

--- a/solution.py
+++ b/solution.py
@@ -101,7 +101,14 @@
             student_states[0, batch_index * batch_rows : (batch_index + 1) * batch_rows],
             student_gain,
         )
-        gathered = lax.all_gather(local_rows, "ctx", axis=0, tiled=True)
+        ring = [local_rows]
+        for hop in range(3):
+            ring.append(lax.ppermute(ring[-1], "ctx", [(dev, (dev + 1) % 4) for dev in range(4)]))
+        gathered = jnp.roll(
+            jnp.concatenate(ring[::-1], axis=0),
+            (lax.axis_index("ctx") + 1) * ring[0].shape[0],
+            axis=0,
+        )
         raw_activation_grid = lax.cond(
             is_teacher,
             lambda rows: jnp.zeros((rows.shape[0], QUANTIZER_TOTAL, columns), jnp.float32),

time: 630 us -> 608 us (0.965)
  blocking collectives: 179 us -> 87.2 us
  waiting for transfers between devices: 274 us -> 322 us
  starting transfers between devices: 3.57 us -> 19.5 us
    all_gather x4 -> x0, blocking collectives: 124 us -> none  [on_device(): gathered = lax.all_gather(local_rows, 'ctx', axis=0, tiled=True)]
    ppermute x0 -> x12, waiting for transfers between devices: none -> 46.5 us  [on_device(): lax.ppermute(ring[-1], 'ctx', [(dev, (dev + 1) % 4) for dev in range(4)])]
    all_gather x1, blocking collectives: 12.5 us -> 45.1 us  [on_device(): lax.all_gather(targets, 'ctx', axis=1, tiled=True)]
    ppermute x0 -> x12, starting transfers between devices: none -> 16.1 us  [on_device(): lax.ppermute(ring[-1], 'ctx', [(dev, (dev + 1) % 4) for dev in range(4)])]
    concatenate x0 -> x4, other arithmetic: none -> 13.5 us  [on_device(): jnp.roll(jnp.concatenate(ring[::-1], axis=0), (lax.axis_index('ctx') + 1)...]
    unnamed x21, waiting for transfers between devices: 74.6 us -> 68.1 us
    unnamed x32 -> x56, local copies, waits for them, and re-layouts: 15.2 us -> 15.5 us
  transfers between devices with their start and end apart: 14 -> 26, of which waited for: 6 -> 13; matrix products, arithmetic and copies ran while one was open for 18% -> 21% of each run, Pallas kernels for 0% -> 0%
where the time goes in v1:
time: 608 us; the launch traced here: 599 us
  waiting for transfers between devices  322 us (53%)
  blocking collectives  87.2 us (14%)
  local copies, waits for them, and re-layouts  61.4 us (10%)
  matrix products  52.1 us (9%)
  other arithmetic  40.5 us (7%)
  starting transfers between devices  19.5 us (3%)
  between operations  14.7 us (2%)
    reduce_scatter x1, waiting for transfers between devices, on_device(): lax.psum_scatter(gradient, ('role', 'dp'), scatter_dimension=1, tiled=True)  182 us
    unnamed x21, waiting for transfers between devices  68.1 us
    cond x4, matrix products, on_device(): lax.cond(is_teacher, lambda piece: jnp.einsum('rd,qdc->rqc', piece, mento...  52 us
    ppermute x12, waiting for transfers between devices, on_device(): lax.ppermute(ring[-1], 'ctx', [(dev, (dev + 1) % 4) for dev in range(4)])  46.5 us
    all_gather x1, blocking collectives, on_device(): lax.all_gather(targets, 'ctx', axis=1, tiled=True)  45.1 us
    cond x1, local copies, waits for them, and re-layouts, on_device(): lax.cond(is_teacher, lambda total: total, lambda total: total + jnp.einsu...  27.6 us
    ppermute x1, waiting for transfers between devices, shifted(): lax.ppermute(value, axis, [(source, source + steps) for source in range(i...  23.3 us
    pmax x1, blocking collectives, on_device(): largest_activation = lax.pmax(local_peak, 'ctx')  16.9 us
  transfers between devices with their start and end apart: 26, of which 13 were waited for; matrix products, arithmetic and copies ran while one was open for 21% of the time, Pallas kernels for 0%

profile of v1, /device:TPU:0, one launch (start us, length us, event | category | flops | bytes accessed | tf_op | source)
XLA Modules:
  0.0 599.0 jit_solution(10661042038938093277)
XLA Ops:
  7.2 1.8 fusion.72
  9.0 2.1 fusion.74
  13.3 3.1 collective-permute-start.4
  16.5 1.6 collective-permute-start.10
  18.0 1.6 collective-permute-start.7
  19.7 5.3 collective-permute-done.4
  25.3 45.1 %all_gather.23 = s32[1,512,4]{1,2,0:T(4,128)S(1)} all-gather(s32[1,128,4]{1,2,0:T(4,128)S(1)} %copy-done.18), channel_id=1, replica_groups=mesh['role'=2,'dp'=4,'ctx'=4] {'ctx'}, dimensions={1}, use_global_device_ids=true | all-gather | bytes 10240 | tf_op jit(solution)/shard_map/all_gather | solution.py:44
  70.4 1.6 collective-permute-start.11
  72.1 1.6 collective-permute-start.1
  73.7 1.7 collective-permute-start.6
  75.9 8.5 %collective-permute-done.11 = bf16[32,3584]{1,0:T(8,128)(2,1)} collective-permute-done((bf16[32,3584]{1,0:T(8,128)(2,1)S(1)}, bf16[32,3584]{1,0:T(8,128)(2,1)}, u32[]{:S(2)}, u32[]{:S(2)}) %collective-permute-start.11) | collective-permute-done | bytes 229408 | tf_op jit(solution)/shard_map/ppermute | solution.py:106
  84.4 1.1 collective-permute-start.12
  85.5 8.6 %collective-permute-done.8 = bf16[32,3584]{1,0:T(8,128)(2,1)S(1)} collective-permute-done((bf16[32,3584]{1,0:T(8,128)(2,1)S(1)}, bf16[32,3584]{1,0:T(8,128)(2,1)S(1)}, u32[]{:S(2)}, u32[]{:S(2)}) %collective-permute-start.8) | collective-permute-done | bytes 229408 | tf_op jit(solution)/shard_map/ppermute | solution.py:106
  94.1 1.8 collective-permute-start.9
  95.9 8.0 %collective-permute-done.1 = bf16[32,3584]{1,0:T(8,128)(2,1)S(1)} collective-permute-done((bf16[32,3584]{1,0:T(8,128)(2,1)S(1)}, bf16[32,3584]{1,0:T(8,128)(2,1)S(1)}, u32[]{:S(2)}, u32[]{:S(2)}) %collective-permute-start.1) | collective-permute-done | bytes 229408 | tf_op jit(solution)/shard_map/ppermute | solution.py:106
  103.9 1.7 collective-permute-start.2
  105.7 8.2 %collective-permute-done.6 = bf16[32,3584]{1,0:T(8,128)(2,1)} collective-permute-done((bf16[32,3584]{1,0:T(8,128)(2,1)S(1)}, bf16[32,3584]{1,0:T(8,128)(2,1)}, u32[]{:S(2)}, u32[]{:S(2)}) %collective-permute-start.6) | collective-permute-done | bytes 229408 | tf_op jit(solution)/shard_map/ppermute | solution.py:106
  113.9 3.1 fusion.61
  117.0 7.9 %collective-permute-done.9 = bf16[32,3584]{1,0:T(8,128)(2,1)S(1)} collective-permute-done((bf16[32,3584]{1,0:T(8,128)(2,1)S(1)}, bf16[32,3584]{1,0:T(8,128)(2,1)S(1)}, u32[]{:S(2)}, u32[]{:S(2)}) %collective-permute-start.9) | collective-permute-done | bytes 229408 | tf_op jit(solution)/shard_map/ppermute | solution.py:106
  124.8 3.2 fusion.54
  128.1 3.2 fusion.68
  131.6 1.4 copy.61
  134.1 1.3 copy.68
  135.4 4.0 fusion.47
  140.0 13.0 %conditional.14 = (f32[128,4,512]{0,2,1:T(8,128)S(1)}) conditional(s32[]{:T(128)} %convert_element_type.149, () %tuple.85, (bf16[128,5120]{1,0:T(8,128)(2,1)}, bf16[4,5120,512]{2,1,0:T(8,128)(2,1)}) %tuple.86), branch_computations={%region_16.0_spmd, %region_17.0_spmd} | conditional | flops 2684354560 | bytes 23330824 | solution.py:74
  140.3 12.7 %fusion.4 = f32[128,4,512]{0,2,1:T(8,128)S(1)} fusion(bf16[4,5120,512]{2,1,0:T(8,128)(2,1)} %get-tuple-element.94, bf16[128,5120]{1,0:T(8,128)(2,1)} %get-tuple-element.92), kind=kOutput, calls=%fused_computation.4 | convolution fusion | flops 2684354560 | bytes 23330816 | tf_op jit(solution)/shard_map/cond | solution.py:74
  153.0 13.8 %conditional.15 = (f32[128,4,512]{0,2,1:T(8,128)}) conditional(s32[]{:T(128)} %convert_element_type.149, () %tuple.87, (bf16[128,5120]{1,0:T(8,128)(2,1)}, bf16[4,5120,512]{2,1,0:T(8,128)(2,1)}) %tuple.88), branch_computations={%region_23.0_spmd, %region_24.0_spmd} | conditional | flops 2684354560 | bytes 23330824 | solution.py:74
  153.1 13.8 %fusion.6 = f32[128,4,512]{0,2,1:T(8,128)} fusion(bf16[4,5120,512]{2,1,0:T(8,128)(2,1)} %get-tuple-element.96, bf16[128,5120]{1,0:T(8,128)(2,1)} %get-tuple-element.95), kind=kOutput, calls=%fused_computation.6 | convolution fusion | flops 2684354560 | bytes 23330816 | tf_op jit(solution)/shard_map/cond | solution.py:74
  166.8 13.1 %conditional.16 = (f32[128,4,512]{0,2,1:T(8,128)S(1)}) conditional(s32[]{:T(128)} %convert_element_type.149, () %tuple.89, (bf16[128,5120]{1,0:T(8,128)(2,1)}, bf16[4,5120,512]{2,1,0:T(8,128)(2,1)}) %tuple.90), branch_computations={%region_30.0_spmd, %region_31.0_spmd} | conditional | flops 2684354560 | bytes 23330824 | solution.py:74
  166.8 12.7 %fusion.8 = f32[128,4,512]{0,2,1:T(8,128)S(1)} fusion(bf16[4,5120,512]{2,1,0:T(8,128)(2,1)} %get-tuple-element.102, bf16[128,5120]{1,0:T(8,128)(2,1)} %get-tuple-element.97), kind=kOutput, calls=%fused_computation.8 | convolution fusion | flops 2684354560 | bytes 23330816 | tf_op jit(solution)/shard_map/cond | solution.py:74
  180.0 1.0 copy-done.2
  181.1 1.3 multiply_reduce_fusion.1
  182.5 2.7 all-gather.5.cloned.1.call-done
  185.2 12.8 %conditional.13 = (f32[128,4,512]{0,2,1:T(8,128)S(1)}) conditional(s32[]{:T(128)} %convert_element_type.149, () %tuple.83, (bf16[128,5120]{1,0:T(8,128)(2,1)}, bf16[4,5120,512]{2,1,0:T(8,128)(2,1)}) %tuple.84), branch_computations={%region_9.0_spmd, %region_10.0_spmd} | conditional | flops 2684354560 | bytes 23330824 | solution.py:74
  185.2 12.8 %fusion.2 = f32[128,4,512]{0,2,1:T(8,128)S(1)} fusion(bf16[4,5120,512]{2,1,0:T(8,128)(2,1)} %get-tuple-element.87, bf16[128,5120]{1,0:T(8,128)(2,1)} %get-tuple-element.86), kind=kOutput, calls=%fused_computation.2 | convolution fusion | flops 2684354560 | bytes 23330816 | tf_op jit(solution)/shard_map/cond | solution.py:74
  198.0 1.0 copy-done.5
  199.0 16.9 %all-reduce.1 = (f32[128,4]{0,1:T(4,128)S(1)}, f32[128,4]{0,1:T(4,128)S(1)}, f32[128,4]{0,1:T(4,128)S(1)}, f32[128,4]{0,1:T(4,128)S(1)}, f32[128,4]{0,1:T(4,128)...) all-reduce(f32[128,4]{0,1:T(4,128)S(1)} %reduce_max.72, ...), channel_id=1, replica_groups=mesh['role'=2,'dp'=4,'ctx'=4] {'ctx'}, use_global_device_ids=true, to_apply=%region_5.7 | all-reduce | flops 4096 | bytes 32768 | tf_op jit(solution)/shard_map/pmax | solution.py:121
  216.2 1.5 exponential_reduce_fusion.8
  217.7 1.5 exponential_reduce_fusion.9
  220.6 15.7 %all-reduce = (f32[128,4]{0,1:T(4,128)S(1)}, f32[128,4]{0,1:T(4,128)S(1)}, f32[128,4]{0,1:T(4,128)S(1)}, f32[128,4]{0,1:T(4,128)S(1)}, f32[128,4]{0,1:T(4,128)S(...) all-reduce(f32[128,4]{0,1:T(4,128)S(1)} %get-tuple-element.142, ...), channel_id=1, replica_groups=mesh['role'=2,'dp'=4,'ctx'=4] {'ctx'}, use_global_device_ids=true, to_apply=%region_37.0 | all-reduce | flops 6144 | bytes 49152 | tf_op jit(solution)/shard_map/psum | solution.py:123
  236.4 1.5 select_reduce_fusion.5
  238.0 1.5 select_reduce_fusion.3
  240.2 1.6 pad_maximum_fusion
  241.7 2.6 collective-permute-start.3
  244.4 9.4 %all_gather.18 = s32[1,512]{1,0:T(1,128)S(1)} all-gather(s32[1,128]{1,0:T(1,128)S(1)} %copy-done.19), channel_id=1, replica_groups=mesh['role'=2,'dp'=4,'ctx'=4] {'ctx'}, dimensions={1}, use_global_device_ids=true | all-gather | bytes 2560 | tf_op jit(solution)/shard_map/all_gather | solution.py:43
  257.8 23.3 %collective-permute-done.3 = bf16[4,128,4,512]{1,3,2,0:T(8,128)(2,1)} collective-permute-done((bf16[4,128,4,512]{1,3,2,0:T(8,128)(2,1)}, bf16[4,128,4,512]{1,3,2,0:T(8,128)(2,1)}, u32[]{:S(2)}, u32[]{:S(2)}) %collective-permute-start.3) | collective-permute-done | bytes 2097184 | tf_op jit(solution)/shard_map/ppermute | solution.py:16
  281.2 3.7 fusion.43
  288.3 4.3 fusion.42
  292.5 1.7 fusion.30
  294.2 13.5 %conditional.20 = (f32[4,3584,512]{1,2,0:T(8,128)}) conditional(s32[]{:T(128)} %convert_element_type.149, (bf16[128,4,512]{0,2,1:T(8,128)(2,1)S(1)}, bf16[128,3584]{1,0:T(8,128)(2,1)}) %tuple.97, () %tuple.98), branch_computations={%region_65.67_spmd, %region_66.68_spmd} | conditional | flops 1879048192 | bytes 30801928 | solution.py:154
  294.3 13.5 %broadcast_in_dim.6 = f32[4,3584,512]{1,2,0:T(8,128)} broadcast(f32[]{:T(128)} %constant.84.clone), dimensions={} | broadcast | bytes 29360132 | tf_op jit(solution)/shard_map/broadcast_in_dim | solution.py:64
  307.8 1.2 copy-done.11
  309.3 27.6 %copy.77 = f32[4,3584,512]{2,1,0:T(8,128)} copy(f32[4,3584,512]{1,2,0:T(8,128)} %get-tuple-element.229) | data formatting | bytes 58720256 | tf_op jit(solution)/shard_map/cond | solution.py:154
  336.9 0.8 copy.79
  337.7 0.8 copy.91
  338.5 0.8 copy.87
  339.3 0.8 copy.83
  340.1 10.1 %reduce-scatter.42.cloned.1.call-done = f32[32,4]{1,0:T(8,128)} async-done(((f32[128,4]{1,0:T(8,128)}), f32[32,4]{1,0:T(8,128)}) %reduce-scatter.42.cloned.1.call-update) | async-done | bytes 528
  350.2 0.8 copy.93
  351.0 18.7 %reduce-scatter.38.cloned.1.call-done = f32[32,4]{1,0:T(8,128)} async-done(((f32[128,4]{1,0:T(8,128)}), f32[32,4]{1,0:T(8,128)}) %reduce-scatter.38.cloned.1.call-update) | async-done | bytes 528
  370.5 18.9 %reduce-scatter.34.cloned.1.call-done = f32[32,4]{1,0:T(8,128)} async-done(((f32[128,4]{1,0:T(8,128)}), f32[32,4]{1,0:T(8,128)}) %reduce-scatter.34.cloned.1.call-update) | async-done | bytes 528
  390.2 18.8 %reduce-scatter.30.cloned.1.call-done = f32[32,4]{1,0:T(8,128)} async-done(((f32[128,4]{1,0:T(8,128)}), f32[32,4]{1,0:T(8,128)}) %reduce-scatter.30.cloned.1.call-update) | async-done | bytes 528
  409.0 0.8 copy.81
  410.4 181.8 %reduce-scatter.26.cloned.1.call-done = f32[4,448,512]{2,1,0:T(8,128)} async-done(((f32[4,3584,512]{2,1,0:T(8,128)}), f32[4,448,512]{2,1,0:T(8,128)}) %reduce-scatter.26.cloned.1.call-update) | async-done | bytes 3670032 | tf_op jit(solution)/shard_map/reduce_scatter | solution.py:165
  (160 shorter events, 17.9 us)
Async XLA Ops:
  7.2 1.9 copy-start.13
  7.2 132.8 %all-gather.7.cloned.1.call-start = ((), (), s32[]{:S(2)}) async-start(), calls=%async_computation.10 | async-start | bytes 1638400 | tf_op jit(solution)/shard_map/all_gather | solution.py:80
  9.0 3.7 copy-start.14
  9.0 4.0 copy-start.17
  11.2 141.8 %all-gather.9.cloned.1.call-start = ((), (), s32[]{:S(2)}) async-start(), calls=%async_computation.11 | async-start | bytes 1638400 | tf_op jit(solution)/shard_map/all_gather | solution.py:80
  11.2 14.1 %copy-start.18 = (s32[1,128,4]{1,2,0:T(4,128)S(1)}, s32[1,128,4]{1,2,0:T(4,128)}, u32[]{:S(2)}) copy-start(s32[1,128,4]{1,2,0:T(4,128)} %param.41) | copy-start | bytes 6148
  11.9 154.9 %all-gather.11.cloned.1.call-start = ((), (), s32[]{:S(2)}) async-start(), calls=%async_computation.12 | async-start | bytes 1638400 | tf_op jit(solution)/shard_map/all_gather | solution.py:80
  12.7 172.5 %all-gather.5.cloned.1.call-start = ((), (), s32[]{:S(2)}) async-start(), calls=%async_computation.9 | async-start | bytes 1638400 | tf_op jit(solution)/shard_map/all_gather | solution.py:80
  13.3 11.7 %collective-permute-start.4 = (bf16[32,3584]{1,0:T(8,128)(2,1)S(1)}, bf16[32,3584]{1,0:T(8,128)(2,1)S(1)}, u32[]{:S(2)}, u32[]{:S(2)}) collective-permute-start(bf16[32,3584]{1,0:T(8,128)(2,1)S(1)} %get-tuple-element.195), channel_id=1, source_target_pairs={{0,1},{1,2},{2,3},{3,0},{4,5},{5,6},{6,7},{7,4},{8,9},{9,10},{10,1... | collective-permute-start | bytes 688136 | tf_op jit(solution)/shard_map/ppermute | solution.py:106
  16.5 54.0 %collective-permute-start.10 = (bf16[32,3584]{1,0:T(8,128)(2,1)S(1)}, bf16[32,3584]{1,0:T(8,128)(2,1)S(1)}, u32[]{:S(2)}, u32[]{:S(2)}) collective-permute-start(bf16[32,3584]{1,0:T(8,128)(2,1)S(1)} %get-tuple-element.194), channel_id=1, source_target_pairs={{0,1},{1,2},{2,3},{3,0},{4,5},{5,6},{6,7},{7,4},{8,9},{9,10},{10,1... | collective-permute-start | bytes 688136 | tf_op jit(solution)/shard_map/ppermute | solution.py:106
  18.0 54.0 %collective-permute-start.7 = (bf16[32,3584]{1,0:T(8,128)(2,1)S(1)}, bf16[32,3584]{1,0:T(8,128)(2,1)S(1)}, u32[]{:S(2)}, u32[]{:S(2)}) collective-permute-start(bf16[32,3584]{1,0:T(8,128)(2,1)S(1)} %get-tuple-element.196), channel_id=1, source_target_pairs={{0,1},{1,2},{2,3},{3,0},{4,5},{5,6},{6,7},{7,4},{8,9},{9,10},{10,1... | collective-permute-start | bytes 688136 | tf_op jit(solution)/shard_map/ppermute | solution.py:106
  19.6 52.5 %collective-permute-start = (bf16[32,3584]{1,0:T(8,128)(2,1)S(1)}, bf16[32,3584]{1,0:T(8,128)(2,1)S(1)}, u32[]{:S(2)}, u32[]{:S(2)}) collective-permute-start(bf16[32,3584]{1,0:T(8,128)(2,1)S(1)} %get-tuple-element.197), channel_id=1, source_target_pairs={{0,1},{1,2},{2,3},{3,0},{4,5},{5,6},{6,7},{7,4},{8,9},{9,10},{10,1... | collective-permute-start | bytes 688136 | tf_op jit(solution)/shard_map/ppermute | solution.py:106
  25.0 48.7 %collective-permute-start.5 = (bf16[32,3584]{1,0:T(8,128)(2,1)S(1)}, bf16[32,3584]{1,0:T(8,128)(2,1)S(1)}, u32[]{:S(2)}, u32[]{:S(2)}) collective-permute-start(bf16[32,3584]{1,0:T(8,128)(2,1)S(1)} %collective-permute-done.4), channel_id=1, source_target_pairs={{0,1},{1,2},{2,3},{3,0},{4,5},{5,6},{6,7},{7,4},{8,9},{9,10},{10,1... | collective-permute-start | bytes 688136 | tf_op jit(solution)/shard_map/ppermute | solution.py:106
  25.2 311.6 %reduce-scatter.28.cloned.1.call-start = ((), (), s32[]{:S(2)}) async-start(), calls=%async_computation.14 | async-start | bytes 81920
  70.4 14.0 %collective-permute-start.11 = (bf16[32,3584]{1,0:T(8,128)(2,1)S(1)}, bf16[32,3584]{1,0:T(8,128)(2,1)}, u32[]{:S(2)}, u32[]{:S(2)}) collective-permute-start(bf16[32,3584]{1,0:T(8,128)(2,1)S(1)} %collective-permute-done.10), channel_id=1, source_target_pairs={{0,1},{1,2},{2,3},{3,0},{4,5},{5,6},{6,7},{7,4},{8,9},{9,10},{10,1... | collective-permute-start | bytes 688136 | tf_op jit(solution)/shard_map/ppermute | solution.py:106
  72.0 22.1 %collective-permute-start.8 = (bf16[32,3584]{1,0:T(8,128)(2,1)S(1)}, bf16[32,3584]{1,0:T(8,128)(2,1)S(1)}, u32[]{:S(2)}, u32[]{:S(2)}) collective-permute-start(bf16[32,3584]{1,0:T(8,128)(2,1)S(1)} %collective-permute-done.7), channel_id=1, source_target_pairs={{0,1},{1,2},{2,3},{3,0},{4,5},{5,6},{6,7},{7,4},{8,9},{9,10},{10,1... | collective-permute-start | bytes 688136 | tf_op jit(solution)/shard_map/ppermute | solution.py:106
  72.1 31.8 %collective-permute-start.1 = (bf16[32,3584]{1,0:T(8,128)(2,1)S(1)}, bf16[32,3584]{1,0:T(8,128)(2,1)S(1)}, u32[]{:S(2)}, u32[]{:S(2)}) collective-permute-start(bf16[32,3584]{1,0:T(8,128)(2,1)S(1)} %collective-permute-done), channel_id=1, source_target_pairs={{0,1},{1,2},{2,3},{3,0},{4,5},{5,6},{6,7},{7,4},{8,9},{9,10},{10,1... | collective-permute-start | bytes 688136 | tf_op jit(solution)/shard_map/ppermute | solution.py:106
  73.7 40.2 %collective-permute-start.6 = (bf16[32,3584]{1,0:T(8,128)(2,1)S(1)}, bf16[32,3584]{1,0:T(8,128)(2,1)}, u32[]{:S(2)}, u32[]{:S(2)}) collective-permute-start(bf16[32,3584]{1,0:T(8,128)(2,1)S(1)} %collective-permute-done.5), channel_id=1, source_target_pairs={{0,1},{1,2},{2,3},{3,0},{4,5},{5,6},{6,7},{7,4},{8,9},{9,10},{10,1... | collective-permute-start | bytes 688136 | tf_op jit(solution)/shard_map/ppermute | solution.py:106
  84.4 51.0 %collective-permute-start.12 = (bf16[32,3584]{1,0:T(8,128)(2,1)}, bf16[32,3584]{1,0:T(8,128)(2,1)}, u32[]{:S(2)}, u32[]{:S(2)}) collective-permute-start(bf16[32,3584]{1,0:T(8,128)(2,1)} %collective-permute-done.11), channel_id=1, source_target_pairs={{0,1},{1,2},{2,3},{3,0},{4,5},{5,6},{6,7},{7,4},{8,9},{9,10},{10,1... | collective-permute-start | bytes 688136 | tf_op jit(solution)/shard_map/ppermute | solution.py:106
  94.1 30.7 %collective-permute-start.9 = (bf16[32,3584]{1,0:T(8,128)(2,1)S(1)}, bf16[32,3584]{1,0:T(8,128)(2,1)S(1)}, u32[]{:S(2)}, u32[]{:S(2)}) collective-permute-start(bf16[32,3584]{1,0:T(8,128)(2,1)S(1)} %collective-permute-done.8), channel_id=1, source_target_pairs={{0,1},{1,2},{2,3},{3,0},{4,5},{5,6},{6,7},{7,4},{8,9},{9,10},{10,1... | collective-permute-start | bytes 688136 | tf_op jit(solution)/shard_map/ppermute | solution.py:106
  103.9 24.1 %collective-permute-start.2 = (bf16[32,3584]{1,0:T(8,128)(2,1)S(1)}, bf16[32,3584]{1,0:T(8,128)(2,1)S(1)}, u32[]{:S(2)}, u32[]{:S(2)}) collective-permute-start(bf16[32,3584]{1,0:T(8,128)(2,1)S(1)} %collective-permute-done.1), channel_id=1, source_target_pairs={{0,1},{1,2},{2,3},{3,0},{4,5},{5,6},{6,7},{7,4},{8,9},{9,10},{10,1... | collective-permute-start | bytes 688136 | tf_op jit(solution)/shard_map/ppermute | solution.py:106
  117.0 16.8 %copy-start.10 = (bf16[128,3584]{1,0:T(8,128)(2,1)}, bf16[128,3584]{1,0:T(8,128)(2,1)S(1)}, u32[]{:S(2)}) copy-start(bf16[128,3584]{1,0:T(8,128)(2,1)S(1)} %fusion.61) | copy-start | bytes 2752516
  153.0 29.4 %copy-start.1 = (f32[128,4,512]{0,2,1:T(8,128)}, f32[128,4,512]{0,2,1:T(8,128)S(1)}, u32[]{:S(2)}) copy-start(f32[128,4,512]{0,2,1:T(8,128)S(1)} %get-tuple-element.124) | copy-start | bytes 3145732
  180.0 1.0 copy-start.2
  185.2 30.8 %copy-start.3 = (f32[128,4,512]{0,2,1:T(8,128)S(1)}, f32[128,4,512]{0,2,1:T(8,128)}, u32[]{:S(2)}) copy-start(f32[128,4,512]{0,2,1:T(8,128)} %copy-done.2) | copy-start | bytes 3145732
  198.0 1.0 copy-start.5
  216.0 3.2 copy-start.6
  216.2 3.3 copy-start.8
  217.7 2.0 copy-start
  236.4 3.1 copy-start.4
  238.0 1.8 copy-start.7
  240.1 4.2 copy-start.19
  241.7 39.4 %collective-permute-start.3 = (bf16[4,128,4,512]{1,3,2,0:T(8,128)(2,1)}, bf16[4,128,4,512]{1,3,2,0:T(8,128)(2,1)}, u32[]{:S(2)}, u32[]{:S(2)}) collective-permute-start(bf16[4,128,4,512]{1,3,2,0:T(8,128)(2,1)} %pad_maximum_fusion), channel_id=1, source_target_pairs={{0,16},{1,17},{2,18},{3,19},{4,20},{5,21},{6,22},{7,23},{8,24},{9,... | collective-permute-start | bytes 6291464 | tf_op jit(solution)/shard_map/ppermute | solution.py:16
  254.7 83.0 %reduce-scatter.40.cloned.1.call-start = ((), (), s32[]{:S(2)}) async-start(), calls=%async_computation.20 | async-start | bytes 81920
  255.6 82.9 %reduce-scatter.36.cloned.1.call-start = ((), (), s32[]{:S(2)}) async-start(), calls=%async_computation.18 | async-start | bytes 81920
  256.5 82.7 %reduce-scatter.32.cloned.1.call-start = ((), (), s32[]{:S(2)}) async-start(), calls=%async_computation.16 | async-start | bytes 81920
  257.7 92.4 %reduce-scatter.42.cloned.1.call-start = ((), (), s32[]{:S(2)}) async-start(), calls=%async_computation.21 | async-start | bytes 81920
  285.6 84.1 %reduce-scatter.38.cloned.1.call-start = ((), (), s32[]{:S(2)}) async-start(), calls=%async_computation.19 | async-start | bytes 81920
  286.4 103.0 %reduce-scatter.34.cloned.1.call-start = ((), (), s32[]{:S(2)}) async-start(), calls=%async_computation.17 | async-start | bytes 81920
  287.2 121.7 %reduce-scatter.30.cloned.1.call-start = ((), (), s32[]{:S(2)}) async-start(), calls=%async_computation.15 | async-start | bytes 81920
  288.0 304.3 %reduce-scatter.26.cloned.1.call-start = ((), (), s32[]{:S(2)}) async-start(), calls=%async_computation.13 | async-start | bytes 33030144 | tf_op jit(solution)/shard_map/reduce_scatter | solution.py:165
  288.2 4.3 copy-start.9
  294.2 13.5 %copy-start.12 = (bf16[128,3584]{1,0:T(8,128)(2,1)S(1)}, bf16[128,3584]{1,0:T(8,128)(2,1)}, u32[]{:S(2)}) copy-start(bf16[128,3584]{1,0:T(8,128)(2,1)} %fusion.54) | copy-start | bytes 2752516
  294.2 13.5 %copy-start.16 = (bf16[128,4,512]{0,2,1:T(8,128)(2,1)S(1)}, bf16[128,4,512]{0,2,1:T(8,128)(2,1)}, u32[]{:S(2)}) copy-start(bf16[128,4,512]{0,2,1:T(8,128)(2,1)} %get-tuple-element.181) | copy-start | bytes 1572868
  307.7 1.2 copy-start.11
  307.7 1.3 copy-start.15
Sparse Core Ops, SparseCore 0:
  11.3 53.8 all-gather.6
  66.8 52.8 all-gather.8
  121.3 30.7 all-gather.10
  153.5 31.6 all-gather.4
  254.8 16.5 reduce-scatter.27
  273.5 17.4 reduce-scatter.39
  293.2 17.4 reduce-scatter.35
  312.9 17.4 reduce-scatter.31
  332.7 17.4 reduce-scatter.41
  352.2 17.4 reduce-scatter.37
  371.9 17.4 reduce-scatter.33
  391.5 17.4 reduce-scatter.29
  413.2 179.0 reduce-scatter.25
